TPU v7x, 128 devices: a whole 4x4x4 slice. The times are simulated.
128 devices in a mesh: expert: 8 (over y, x_lo), ffn: 16 (over z, x_hi, core).
Axes of the slice: x: 4 (x_hi: 2, x_lo: 2; x = x_hi * 2 + x_lo), y: 4, z: 4, core: 2. Of those that a mesh axis runs over, the one named last changes fastest.
Arguments:
- tokens: bfloat16 [2048, 4096], P('expert'), may hold values from -6 to 6
- router_gates: float32 [2048, 2], P('expert'), may hold values from 0.1 to 1
- routes: int32 [2048, 2], P('expert'), may hold values from 0 to 7, all different within a row; in each aligned block of 256 rows (0 to 255, 256 to 511, ...) at most 128 rows name the same one
- gate_proj: bfloat16 [8, 4096, 14336], P('expert', None, 'ffn'), may hold values from -0.09375 to 0.09375
- up_proj: bfloat16 [8, 4096, 14336], P('expert', None, 'ffn'), may hold values from -0.09375 to 0.09375
- down_proj: bfloat16 [8, 14336, 4096], P('expert', 'ffn'), may hold values from -0.0625 to 0.0625
Outputs:
- mixed: bfloat16 [2048, 4096], P('expert', 'ffn')
Inputs may be any that keep to these rules, and one draw needn't show every extreme that they name: `routes`: the 2 experts of a token differ. Among the tokens of one index of the expert axis (aligned blocks of 256 tokens) no expert is chosen by more than 128 tokens, and in some blocks one expert is chosen by exactly 128.
All inputs are finite; a program needn't handle non-finite values.
Results may differ from a plain program's by a relative error of at most 0.017.
Values may be sent and summed in bfloat16 or wider, within the bound.
A program may use at most 128 MiB of HBM per device.

v0:
```python
import jax
import jax.numpy as jnp
from jax import lax
from jax.sharding import PartitionSpec as P

TOP = 2


def per_device(tokens, router_gates, routes, gate_proj, up_proj, down_proj):
    experts = lax.axis_size("expert")
    groups = lax.axis_size("ffn")
    tok_rows = tokens.shape[0]
    width_all = tokens.shape[1]
    capacity = 2 * TOP * tok_rows // experts
    slots_all = experts * capacity
    col_width = width_all // groups
    gate_matrix = gate_proj[0]
    up_matrix = up_proj[0]
    down_matrix = down_proj[0]
    flattened = routes.reshape(-1)
    chosen = (flattened[:, None] == jnp.arange(experts, dtype=jnp.int32)[None, :]).astype(jnp.int32)
    ranking = jnp.cumsum(chosen, axis=0) - chosen
    targets = (flattened * capacity + jnp.sum(ranking * chosen, axis=1)).reshape(tok_rows, TOP)
    slot_ids = jnp.arange(slots_all, dtype=jnp.int32)
    matches = targets[:, :, None] == slot_ids[None, None, :]
    placing = jnp.any(matches, axis=1).astype(jnp.bfloat16)
    weighting = jnp.sum(jnp.where(matches, router_gates[:, :, None], 0.0), axis=1)
    outgoing = lax.dot_general(
        placing, tokens, (((0,), (0,)), ((), ())), preferred_element_type=jnp.float32
    )
    outgoing = outgoing.astype(jnp.bfloat16).reshape(experts, capacity, width_all)
    own_columns = lax.dynamic_slice_in_dim(
        outgoing, lax.axis_index("ffn") * col_width, col_width, 2
    )
    landed = lax.all_to_all(own_columns, "expert", split_axis=0, concat_axis=0, tiled=True)
    shard_piece = lax.all_gather(landed, "ffn", axis=2, tiled=True)
    row_count = shard_piece.shape[2]
    flat_rows = shard_piece.reshape(slots_all, row_count)
    gate_act = jnp.dot(flat_rows, gate_matrix, preferred_element_type=jnp.float32)
    up_act = jnp.dot(flat_rows, up_matrix, preferred_element_type=jnp.float32)
    hidden = (jax.nn.silu(gate_act) * up_act).astype(jnp.bfloat16)
    summed = lax.psum_scatter(
        lax.dot_general(
            down_matrix, hidden, (((0,), (1,)), ((), ())), preferred_element_type=jnp.float32
        ).astype(jnp.bfloat16),
        "ffn",
        scatter_dimension=0,
        tiled=True,
    ).astype(jnp.float32)
    returned_rows = lax.all_to_all(
        summed.reshape(col_width, experts, capacity).astype(jnp.bfloat16),
        "expert",
        split_axis=1,
        concat_axis=1,
        tiled=True,
    ).astype(jnp.float32)
    mixed = lax.dot_general(
        weighting,
        returned_rows.reshape(col_width, slots_all),
        (((1,), (1,)), ((), ())),
        preferred_element_type=jnp.float32,
    )
    return mixed.astype(jnp.bfloat16)


def solution(mesh):
    in_specs = (
        P("expert", None),
        P("expert", None),
        P("expert", None),
        P("expert", None, "ffn"),
        P("expert", None, "ffn"),
        P("expert", "ffn", None),
    )
    out_specs = P("expert", "ffn")
    return jax.shard_map(
        per_device, mesh=mesh, in_specs=in_specs, out_specs=out_specs, check_vma=False
    )
```

profile of v0, /device:TPU:0, one launch (start us, length us, event | category | flops | bytes accessed | tf_op | source)
XLA Modules:
  0.0 265.9 jit_solution(985346385771714625)
XLA Ops:
  6.5 1.0 copy.19
  7.5 0.1 eq.42
  7.7 0.1 eq.38
  7.8 1.1 reduce-window.6
  9.0 0.2 slice_reduce_fusion
  9.2 0.1 fusion.9
  9.3 0.1 reduce_sum.21
  9.5 0.1 copy.21
  9.5 0.7 multiply_add_fusion
  10.2 0.3 fusion.7
  10.5 5.6 %convolution_convert_fusion = bf16[1024,4096]{1,0:T(8,128)(2,1)} fusion(pred[256,1024]{1,0:T(8,128)(4,1)S(1)} %fusion.7, bf16[256,4096]{1,0:T(8,128)(2,1)S(1)} %copy-done), kind=kOutput, calls=%fused_computation.1 | convolution fusion | flops 2151677952 | bytes 10747904 | tf_op jit(solution)/shard_map/dot_general | solution.py:28
  16.1 1.1 constant_dynamic-slice_fusion
  17.2 15.5 %all_to_all.10 = bf16[8,128,256]{2,1,0:T(8,128)(2,1)} all-to-all(bf16[8,128,256]{2,1,0:T(8,128)(2,1)S(1)} %constant_dynamic-slice_fusion), channel_id=1, replica_groups=mesh['expert'=8,'ffn'=16] {'expert'}, dimensions={0} | all-to-all | bytes 1048576 | tf_op jit(solution)/shard_map/all_to_all | solution.py:35
  32.7 0.0 all-gather.2.cloned.1.call-update
  32.8 0.2 reduce-scatter.2.cloned.1.call-start
  33.0 76.5 %all-gather.2.cloned.1.call-done = bf16[8,128,4096]{2,1,0:T(8,128)(2,1)} async-done(((bf16[8,128,256]{2,1,0:T(8,128)(2,1)}), bf16[8,128,4096]{2,1,0:T(8,128)(2,1)}) %all-gather.2.cloned.1.call-update) | async-done | bytes 8388624 | tf_op jit(solution)/shard_map/all_gather | solution.py:36
  109.5 12.5 %fusion.1 = f32[1024,896]{1,0:T(8,128)S(1)} fusion(bf16[1024,4096]{1,0:T(8,128)(2,1)} %bitcast.35, bf16[1,4096,896]{2,1,0:T(8,128)(2,1)} %param.10), kind=kOutput, calls=%fused_computation.3 | convolution fusion | flops 7516192768 | bytes 19398656 | tf_op jit(solution)/shard_map/dot_general | solution.py:40
  122.0 12.0 %multiply_convert_fusion = bf16[1024,896]{1,0:T(8,128)(2,1)S(1)} fusion(f32[1024,896]{1,0:T(8,128)S(1)} %fusion.1, bf16[1024,4096]{1,0:T(8,128)(2,1)S(1)} %bitcast.36, bf16[1,4096,896]{2,1,0:T(8,128)(2,1)} %param.9), kind=kOutput, calls=%fused_computation.7 | convolution fusion | flops 7521697792 | bytes 21233664 | tf_op jit(solution)/shard_map/dot_general | solution.py:39
  134.0 11.1 %convert_bitcast_fusion = bf16[4096,1024]{0,1:T(8,128)(2,1)} fusion(bf16[1024,896]{1,0:T(8,128)(2,1)S(1)} %multiply_convert_fusion, bf16[1,896,4096]{2,1,0:T(8,128)(2,1)S(1)} %bitcast.38), kind=kOutput, calls=%fused_computation | convolution fusion | flops 7520387072 | bytes 17563648 | tf_op jit(solution)/shard_map/dot_general | solution.py:43
  145.2 99.8 %reduce-scatter.2.cloned.1.call-done = bf16[256,1024]{0,1:T(8,128)(2,1)} async-done(((bf16[4096,1024]{0,1:T(8,128)(2,1)}), bf16[256,1024]{0,1:T(8,128)(2,1)}) %reduce-scatter.2.cloned.1.call-update) | async-done | bytes 524304 | tf_op jit(solution)/shard_map/reduce_scatter | solution.py:42
  245.0 4.3 %all-to-all-start.1 = ((bf16[256,8,128]{0,2,1:T(8,128)(2,1)}), bf16[256,8,128]{0,2,1:T(8,128)(2,1)S(1)}, u32[]{:S(2)}, u32[]{:S(2)}) async-start(bf16[256,8,128]{0,2,1:T(8,128)(2,1)} %bitcast.34), calls=%async_computation.2 | async-start | bytes 1048576 | tf_op jit(solution)/shard_map/all_to_all | solution.py:50
  249.3 0.3 select_reduce_fusion
  249.6 8.5 %all-to-all-done.1 = bf16[256,8,128]{0,2,1:T(8,128)(2,1)S(1)} async-done(((bf16[256,8,128]{0,2,1:T(8,128)(2,1)}), bf16[256,8,128]{0,2,1:T(8,128)(2,1)S(1)}, u32[]{:S(2)}, u32[]{:S(2)}) %all-to-all-start.1) | async-done | bytes 524320 | tf_op jit(solution)/shard_map/all_to_all | solution.py:50
  258.1 1.0 fusion.11
  (16 shorter events, 0.1 us)
Async XLA Ops:
  6.5 4.0 %copy-start = (bf16[256,4096]{1,0:T(8,128)(2,1)S(1)}, bf16[256,4096]{1,0:T(8,128)(2,1)}, u32[]{:S(2)}) copy-start(bf16[256,4096]{1,0:T(8,128)(2,1)} %param.6) | copy-start | bytes 6291460
  6.5 102.9 %all-gather.2.cloned.1.call-start = ((), (), s32[]{:S(2)}) async-start(), calls=%async_computation.3 | async-start | bytes 8912896 | tf_op jit(solution)/shard_map/all_gather | solution.py:36
  32.8 212.2 %reduce-scatter.2.cloned.1.call-start = ((), (), s32[]{:S(2)}) async-start(), calls=%async_computation.4 | async-start | bytes 8912896 | tf_op jit(solution)/shard_map/reduce_scatter | solution.py:42
  109.5 12.5 %copy-start.2 = (bf16[8,128,4096]{2,1,0:T(8,128)(2,1)S(1)}, bf16[8,128,4096]{2,1,0:T(8,128)(2,1)}, u32[]{:S(2)}) copy-start(bf16[8,128,4096]{2,1,0:T(8,128)(2,1)} %all-gather.2.cloned.1.call-done) | copy-start | bytes 25165828
  109.5 24.5 %slice-start = ((s8[7340032]{0:T(1024)(128)(4,1)}), s8[4194304]{0:T(1024)(128)(4,1)S(1)}, s32[]{:S(2)}) async-start(s8[7340032]{0:T(1024)(128)(4,1)} %bitcast.37), calls=%async_computation.5 | async-start | bytes 8388608
  122.0 12.0 %slice-start.1 = ((s8[7340032]{0:T(1024)(128)(4,1)}), s8[3145728]{0:T(1024)(128)(4,1)S(1)}, s32[]{:S(2)}) async-start(s8[7340032]{0:T(1024)(128)(4,1)} %bitcast.37), calls=%async_computation.6 | async-start | bytes 6291456
  145.1 104.1 %copy-start.1 = (f32[256,2]{0,1:T(2,128)S(1)}, f32[256,2]{0,1:T(2,128)}, u32[]{:S(2)}) copy-start(f32[256,2]{0,1:T(2,128)} %param.7) | copy-start | bytes 6148
  245.0 13.1 %all-to-all-start.1 = ((bf16[256,8,128]{0,2,1:T(8,128)(2,1)}), bf16[256,8,128]{0,2,1:T(8,128)(2,1)S(1)}, u32[]{:S(2)}, u32[]{:S(2)}) async-start(bf16[256,8,128]{0,2,1:T(8,128)(2,1)} %bitcast.34), calls=%async_computation.2 | async-start | bytes 1048576 | tf_op jit(solution)/shard_map/all_to_all | solution.py:50
Sparse Core Ops, SparseCore 0:
  32.9 76.5 all-gather.1
  145.3 99.6 reduce-scatter.1
where the time goes:
time: 266 us
  waiting for transfers between devices  185 us (70%)
  matrix products  42.2 us (16%)
  blocking collectives  15.5 us (6%)
  between operations  13.5 us (5%)
  starting transfers between devices  4.52 us (2%)
  local copies, waits for them, and re-layouts  2.78 us (1%)
    reduce_scatter x1, waiting for transfers between devices, per_device(): lax.psum_scatter(lax.dot_general(down_matrix, hidden, (((0,), (1,)), ((),...  99.8 us
    all_gather x1, waiting for transfers between devices, per_device(): shard_piece = lax.all_gather(landed, 'ffn', axis=2, tiled=True)  76.5 us
    all_to_all x1, blocking collectives, per_device(): lax.all_to_all(own_columns, 'expert', split_axis=0, concat_axis=0, tiled=...  15.5 us
    dot_general x1, matrix products, per_device(): up_act = jnp.dot(flat_rows, up_matrix, preferred_element_type=jnp.float32)  12.5 us
    dot_general x1, matrix products, per_device(): jnp.dot(flat_rows, gate_matrix, preferred_element_type=jnp.float32)  12 us
    dot_general x1, matrix products, per_device(): lax.dot_general(down_matrix, hidden, (((0,), (1,)), ((), ())), preferred_...  11.1 us
    all_to_all x1, waiting for transfers between devices, per_device(): lax.all_to_all(summed.reshape(col_width, experts, capacity).astype(jnp.bf...  8.49 us
    dot_general x1, matrix products, per_device(): lax.dot_general(placing, tokens, (((0,), (0,)), ((), ())), preferred_elem...  5.61 us
  transfers between devices with their start and end apart: 3, of which 3 were waited for; matrix products, arithmetic and copies ran while one was open for 0% of the time, Pallas kernels for 0%

commit v1 on v0

v1 whole, which is shorter than its diff:
```python
import jax
import jax.numpy as jnp
from jax import lax
from jax.experimental import pallas as pl
from jax.experimental.pallas import tpu as pltpu
from jax.sharding import PartitionSpec as P

TOP = 2
MESH = pl.DeviceIdType.MESH
REL = ((0, 0), (0, 1), (1, 0), (3, 0), (1, 1), (3, 1), (2, 0), (2, 1))
CHUNKS = ((0, 1), (2, 3), (6, 7), (4, 5))
F32 = jnp.float32
BF16 = jnp.bfloat16


def dot(a, b):
    return jnp.dot(a, b, preferred_element_type=F32)


def kernel(
    tok_hbm, placing, weighting, gate_hbm, up_hbm, down_hbm, out_ref,
    X, Wg, Wu, Wd, tok, OB, OP, hid, part, rD, rA1, rA2, rAx, rBx, rB1, rB2, G,
    send_sem, recv_sem, local_sem,
):
    e = lax.axis_index("expert")
    f = lax.axis_index("ffn")
    y, xl = e // 2, e % 2
    z, xh, c = f // 4, (f // 2) % 2, f % 2
    x = xh * 2 + xl

    def at(yy, xx, zz, cc):
        yy, xx, zz = yy % 4, xx % 4, zz % 4
        return {"expert": yy * 2 + xx % 2, "ffn": zz * 4 + (xx // 2) * 2 + cc}

    loads = [
        pltpu.make_async_copy(s, d, local_sem.at[i])
        for i, (s, d) in enumerate(((tok_hbm, tok), (gate_hbm, Wg), (up_hbm, Wu), (down_hbm, Wd)))
    ]
    for cp in loads:
        cp.start()

    barrier = pltpu.get_barrier_semaphore()
    peers = [
        at(y, x, z, 1 - c), at(y, x + 1, z, c), at(y, x + 3, z, c), at(y, x + 2, z, c),
        at(y + 1, x, z, c), at(y + 3, x, z, c), at(y + 2, x, z, c),
        at(y + 1, x + 1, z, c), at(y + 1, x + 3, z, c), at(y + 3, x + 1, z, c), at(y + 3, x + 3, z, c),
        at(y + 2, x + 1, z, c), at(y + 2, x + 3, z, c), at(y, x, z + 1, c), at(y, x, z + 3, c),
    ]
    for dev in peers:
        pl.semaphore_signal(barrier, inc=1, device_id=dev, device_id_type=MESH)
    pl.semaphore_wait(barrier, len(peers))

    copies = []

    def send(src, dst, dev):
        i = len(copies)
        cp = pltpu.make_async_remote_copy(
            src_ref=src, dst_ref=dst, send_sem=send_sem.at[i], recv_sem=recv_sem.at[i],
            device_id=dev, device_id_type=MESH,
        )
        cp.start()
        copies.append(cp)
        return cp

    other = at(y, x, z, 1 - c)
    half = pl.multiple_of(c * 2048, 2048)

    loads[0].wait()

    def place(t, carry):
        o = pl.multiple_of(t * 512, 512)
        v = dot(placing[128:768, :], tok[:, pl.ds(pl.multiple_of(half + o, 512), 512)])
        OB[:, pl.ds(o, 512)] = v.astype(BF16)
        return carry

    lax.fori_loop(0, 4, place, 0)
    x7 = (x + 1 + 2 * c) % 4
    block = c * 8 + z * 2 + xh
    block7 = c * 8 + z * 2 + x7 // 2

    def cols(b, width=256):
        return pl.ds(pl.multiple_of(b * 256, 256), width)

    OP[0] = dot(placing[768:896, :], tok[:, cols(block)]).astype(BF16)
    OP[1] = dot(placing[896:1024, :], tok[:, cols(block7)]).astype(BF16)

    def quarters(r, yy):
        got = []
        for i, step in enumerate((1, 3)):
            got.append(send(
                OB.at[(r - 1) * 128:r * 128, i * 1024:(i + 1) * 1024],
                X.at[r * 128:(r + 1) * 128, pl.ds(pl.multiple_of(half + i * 1024, 1024), 1024)],
                at(yy, x + step, z, c),
            ))
        return got

    def halves(r, yy):
        return [send(
            OB.at[(r - 1) * 128:r * 128, :],
            X.at[r * 128:(r + 1) * 128, pl.ds(half, 2048)],
            at(yy, x, z, c),
        )]

    arrive = {}
    arrive[1] = quarters(1, y)
    arrive[6] = [send(OP.at[0], X.at[768:896, cols(block)], at(y + 2, x, z, c))]
    arrive[7] = [send(OP.at[1], X.at[896:1024, cols(block7)], at(y + 2, x7, z, c))]
    arrive[2] = halves(2, y + 3)
    arrive[3] = halves(3, y + 1)
    arrive[4] = quarters(4, y + 3)
    arrive[5] = quarters(5, y + 1)

    def place_own(t, carry):
        o = pl.ds(pl.multiple_of(t * 512, 512), 512)
        X[0:128, o] = dot(placing[0:128, :], tok[:, o]).astype(BF16)
        return carry

    lax.fori_loop(0, 8, place_own, 0)

    def landed(cps):
        for cp in cps:
            cp.wait_recv()

    def forward(r):
        landed(arrive[r])
        where = X.at[r * 128:(r + 1) * 128, pl.ds(half, 2048)]
        return send(where, where, other)

    def spread(b, width, dev):
        where = X.at[768:1024, cols(b, width)]
        return send(where, where, dev)

    pair = lambda zz: c * 8 + (zz % 4) * 2
    xdev, up_z, dn_z = at(y, x + 2, z, c), at(y, x, z + 1, c), at(y, x, z + 3, c)

    landed(arrive[6] + arrive[7])
    ag1 = spread(block, 256, xdev)
    fwd1 = forward(1)
    ag1.wait_recv()
    ag2 = [spread(pair(z), 512, up_z), spread(pair(z), 512, dn_z)]
    core_pairs = [spread(pair(z), 512, other)]

    def gather_far():
        landed(ag2)
        far = [spread(pair(z + 3), 256, up_z), spread(pair(z + 1) + 1, 256, dn_z)]
        core_pairs.append(spread(pair(z + 1), 512, other))
        core_pairs.append(spread(pair(z + 3), 512, other))
        return far

    def gather_end(far):
        landed(far)
        core_pairs.append(spread(pair(z + 2), 512, other))

    def gate_up(k, lo, hi):
        row = CHUNKS[k][0] * 128
        rows = slice(row, row + 256)

        def tile(t, carry):
            o = cols(t)
            g = dot(X[rows, :], Wg[:, o])
            u = dot(X[rows, :], Wu[:, o])
            hid[:, o] = (g / (1.0 + jnp.exp(-g)) * u).astype(BF16)
            return carry

        lax.fori_loop(lo, min(hi, 3), tile, 0)
        if hi > 3:
            w = jnp.concatenate([Wg[:, 768:896], Wu[:, 768:896]], axis=1)
            gu = dot(X[rows, :], w)
            g, u = gu[:, :128], gu[:, 128:]
            hid[:, 768:896] = (g / (1.0 + jnp.exp(-g)) * u).astype(BF16)

    def down(k, cc):
        def tile(t, carry):
            for zi in range(2):
                for xi in range(2):
                    zz = t * 2 + zi
                    v = dot(hid[...], Wd[:, cols(zz * 4 + xi * 2 + cc)])
                    part[k, cc, zz, xi] = v.astype(BF16)
            return carry

        lax.fori_loop(0, 2, tile, 0)

    def add(dst, *srcs):
        total = dst[...].astype(F32)
        for s in srcs:
            total = total + s[...].astype(F32)
        dst[...] = total.astype(BF16)

    zp, zm, zf = (z + 1) % 4, (z + 3) % 4, (z + 2) % 4
    st = [dict() for _ in CHUNKS]

    def send_core(k):
        st[k]["d"] = send(part.at[k, 1 - c], rD.at[k], other)

    def s0(k):
        st[k]["d"].wait_recv()

        def body(zz, carry):
            for xi in range(2):
                add(part.at[k, c, zz, xi], rD.at[k, zz, xi])
            return carry

        lax.fori_loop(0, 4, body, 0)
        mine = part.at[k, c]
        st[k]["bx"] = send(mine.at[:, 1 - xh, 128:256], rBx.at[k], xdev)
        st[k]["a1"] = [
            send(mine.at[zf, 0, 0:128], rA1.at[k, 0], up_z),
            send(mine.at[zf, 1, 0:128], rA1.at[k, 1], dn_z),
        ]

    def s1(k):
        mine = part.at[k, c]
        landed(st[k]["a1"])
        add(mine.at[zp, 0, 0:128], rA1.at[k, 0])
        add(mine.at[zm, 1, 0:128], rA1.at[k, 1])
        st[k]["a2"] = [
            send(mine.at[zp, :, 0:128], rA2.at[k, 0], up_z),
            send(mine.at[zm, :, 0:128], rA2.at[k, 1], dn_z),
        ]
        st[k]["bx"].wait_recv()

        def body(zz, carry):
            add(mine.at[zz, xh, 128:256], rBx.at[k, zz])
            return carry

        lax.fori_loop(0, 4, body, 0)
        st[k]["b1"] = [
            send(mine.at[zf, xh, 128:192], rB1.at[k, 0], up_z),
            send(mine.at[zf, xh, 192:256], rB1.at[k, 1], dn_z),
        ]

    def s2(k):
        mine = part.at[k, c]
        landed(st[k]["a2"])
        add(mine.at[z, 1 - xh, 0:128], rA2.at[k, 0, 1 - xh], rA2.at[k, 1, 1 - xh])
        st[k]["ax"] = send(mine.at[z, 1 - xh, 0:128], rAx.at[k], xdev)
        landed(st[k]["b1"])
        add(mine.at[zp, xh, 128:192], rB1.at[k, 0])
        add(mine.at[zm, xh, 192:256], rB1.at[k, 1])
        st[k]["b2"] = [
            send(mine.at[zp, xh, 128:256], rB2.at[k, 0], up_z),
            send(mine.at[zm, xh, 128:256], rB2.at[k, 1], dn_z),
        ]

    returned = []

    def give_back(r, src):
        dy, dx = REL[r]
        if dy == 0 and dx == 0:
            G[r] = src[...]
            return
        owner = {"expert": ((y + dy) % 4) * 2 + (xl + dx) % 2, "ffn": f}
        returned.append(send(src, G.at[r], owner))

    def s3(k):
        mine = part.at[k, c]
        st[k]["ax"].wait_recv()
        add(mine.at[z, xh, 0:128], rA2.at[k, 0, xh], rA2.at[k, 1, xh], rAx.at[k])
        give_back(CHUNKS[k][0], mine.at[z, xh, 0:128])
        landed(st[k]["b2"])
        add(mine.at[z, xh, 128:256], rB2.at[k, 0], rB2.at[k, 1])
        give_back(CHUNKS[k][1], mine.at[z, xh, 128:256])

    loads[1].wait()
    loads[2].wait()
    fwd1.wait_recv()
    gate_up(0, 0, 4)
    loads[3].wait()
    down(0, 1 - c)
    send_core(0)
    down(0, c)
    fwd2 = [forward(2), forward(3)]
    far = gather_far()
    s0(0)
    landed(fwd2)
    gate_up(1, 0, 4)
    gather_end(far)
    s1(0)
    down(1, 1 - c)
    send_core(1)
    down(1, c)
    s2(0)
    s0(1)
    landed(core_pairs)
    gate_up(2, 0, 4)
    fwd3 = [forward(4), forward(5)]
    s3(0)
    s1(1)
    down(2, 1 - c)
    send_core(2)
    down(2, c)
    s2(1)
    s0(2)
    landed(fwd3)
    gate_up(3, 0, 2)
    s3(1)
    s1(2)
    gate_up(3, 2, 4)
    down(3, 1 - c)
    send_core(3)
    s2(2)
    down(3, c)
    s0(3)
    s3(2)
    s1(3)
    s2(3)
    s3(3)
    landed(returned)
    total = jnp.zeros(out_ref.shape, F32)
    for r in range(8):
        w = weighting[:, r * 128:(r + 1) * 128]
        hi = w.astype(BF16)
        lo = (w - hi.astype(F32)).astype(BF16)
        total = total + dot(hi, G[r]) + dot(lo, G[r])
    out_ref[...] = total.astype(BF16)
    for cp in copies:
        cp.wait_send()


N_COPIES = 80


def per_device(tokens, router_gates, routes, gate_proj, up_proj, down_proj):
    experts = lax.axis_size("expert")
    tok_rows, width = tokens.shape
    capacity = 2 * TOP * tok_rows // experts
    hidden = gate_proj.shape[2]
    e = lax.axis_index("expert")
    y, xl = e // 2, e % 2
    flattened = routes.reshape(-1)
    chosen = (flattened[:, None] == jnp.arange(experts, dtype=jnp.int32)[None, :]).astype(jnp.int32)
    ranking = jnp.cumsum(chosen, axis=0) - chosen
    targets = (flattened * capacity + jnp.sum(ranking * chosen, axis=1)).reshape(tok_rows, TOP)
    owners = jnp.stack([((y - dy) % 4) * 2 + (xl + dx) % 2 for dy, dx in REL]).astype(jnp.int32)
    slot_ids = (owners[:, None] * capacity + jnp.arange(capacity, dtype=jnp.int32)[None, :]).reshape(-1)
    first, second = targets[:, 0], targets[:, 1]
    placing = ((slot_ids[:, None] == first[None, :]) | (slot_ids[:, None] == second[None, :])).astype(BF16)
    weighting = jnp.where(first[:, None] == slot_ids[None, :], router_gates[:, 0:1], 0.0) + jnp.where(
        second[:, None] == slot_ids[None, :], router_gates[:, 1:2], 0.0
    )
    vmem = lambda *shape: pltpu.VMEM(shape, BF16)
    any_spec = pl.BlockSpec(memory_space=pl.ANY)
    vmem_spec = pl.BlockSpec(memory_space=pltpu.VMEM)
    return pl.pallas_call(
        kernel,
        out_shape=jax.ShapeDtypeStruct((tok_rows, 256), BF16),
        in_specs=[any_spec, vmem_spec, vmem_spec, any_spec, any_spec, any_spec],
        out_specs=vmem_spec,
        scratch_shapes=[
            vmem(1024, width), vmem(width, hidden), vmem(width, hidden), vmem(hidden, width),
            vmem(tok_rows, width), vmem(640, 2048), vmem(2, 128, 256), vmem(256, hidden),
            vmem(4, 2, 4, 2, 256, 256), vmem(4, 4, 2, 256, 256),
            vmem(4, 2, 128, 256), vmem(4, 2, 2, 128, 256), vmem(4, 128, 256),
            vmem(4, 4, 128, 256), vmem(4, 2, 64, 256), vmem(4, 2, 128, 256), vmem(8, 128, 256),
            pltpu.SemaphoreType.DMA((N_COPIES,)), pltpu.SemaphoreType.DMA((N_COPIES,)),
            pltpu.SemaphoreType.DMA((4,)),
        ],
        compiler_params=pltpu.CompilerParams(
            collective_id=0, has_side_effects=True, vmem_limit_bytes=67043328
        ),
        name="layer",
    )(tokens, placing, weighting, gate_proj[0], up_proj[0], down_proj[0])


def solution(mesh):
    in_specs = (
        P("expert", None),
        P("expert", None),
        P("expert", None),
        P("expert", None, "ffn"),
        P("expert", None, "ffn"),
        P("expert", "ffn", None),
    )
    out_specs = P("expert", "ffn")
    return jax.shard_map(
        per_device, mesh=mesh, in_specs=in_specs, out_specs=out_specs, check_vma=False
    )
```

time: 266 us -> 120 us (0.45)
  waiting for transfers between devices: 185 us -> 0 us
  Pallas kernels: 0 us -> 112 us
  matrix products: 42.2 us -> 0 us
  blocking collectives: 15.5 us -> 0 us
  between operations: 13.5 us -> 0.05 us
  starting transfers between devices: 4.52 us -> 0 us
    pallas_call x0 -> x1, Pallas kernels: none -> 112 us  [per_device(): pl.pallas_call(kernel, out_shape=jax.ShapeDtypeStruct((tok_rows, 256), BF...]
    reduce_scatter x1 -> x0, waiting for transfers between devices: 99.8 us -> none  [per_device(): lax.psum_scatter(lax.dot_general(down_matrix, hidden, (((0,), (1,)), ((),...]
    all_gather x1 -> x0, waiting for transfers between devices: 76.5 us -> none  [per_device(): shard_piece = lax.all_gather(landed, 'ffn', axis=2, tiled=True)]
    dot_general x5 -> x0, matrix products: 42.2 us -> none  [the longest x1 12.5 us: per_device(): up_act = jnp.dot(flat_rows, up_matrix, preferred_element_type=jnp.float32)]
    all_to_all x1 -> x0, blocking collectives: 15.5 us -> none  [per_device(): lax.all_to_all(own_columns, 'expert', split_axis=0, concat_axis=0, tiled=...]
    all_to_all x1 -> x0, waiting for transfers between devices: 8.49 us -> none  [per_device(): lax.all_to_all(summed.reshape(col_width, experts, capacity).astype(jnp.bf...]
    all_to_all x1 -> x0, starting transfers between devices: 4.3 us -> none  [per_device(): lax.all_to_all(summed.reshape(col_width, experts, capacity).astype(jnp.bf...]
  transfers between devices with their start and end apart: 3 -> 0, of which waited for: 3 -> 0; matrix products, arithmetic and copies ran while one was open for 0% -> 0% of each run, Pallas kernels for 0% -> 0%
where the time goes in v1:
time: 120 us
  Pallas kernels  112 us (93%)
  other arithmetic  4.31 us (4%)
  local copies, waits for them, and re-layouts  3.95 us (3%)
    pallas_call x1, Pallas kernels, per_device(): pl.pallas_call(kernel, out_shape=jax.ShapeDtypeStruct((tok_rows, 256), BF...  112 us

profile of v1, /device:TPU:0, one launch (start us, length us, event | category | flops | bytes accessed | tf_op | source)
XLA Modules:
  0.0 119.9 jit_solution(5649079312664387517)
XLA Ops:
  0.0 0.1 stack.35
  0.1 0.8 fusion.3
  0.9 0.1 add_bitcast_fusion
  0.9 0.8 copy.15
  1.7 0.1 eq.100
  1.9 0.1 eq.96
  2.0 1.1 reduce-window.6
  3.2 0.2 slice_reduce_fusion
  3.4 0.1 fusion.1
  3.5 0.1 reduce_sum.12
  3.7 0.1 copy.17
  3.8 0.7 multiply_add_fusion
  4.5 1.0 or_convert_fusion.placing
  5.5 1.2 %select_add_fusion.weighting = f32[256,1024]{1,0:T(8,128)} fusion(f32[256]{0:T(256)S(1)} %bitcast.33, f32[256]{0:T(256)S(1)} %bitcast.32, s32[1024]{0:T(1024)S(1)} %add_bitcast_fusion, s32[256]{0:T(256)S(1)} %bitcast.31, s32[256]{0:T(256)S(1)} %bitcast.29), kind=kLoop, calls=%fused_computation | loop fusion | flops 1310720 | bytes 1056768 | tf_op jit(solution)/shard_map/add | solution.py:338
  6.7 111.6 %layer.1 = bf16[256,256]{1,0:T(8,128)(2,1)} custom-call(bf16[256,4096]{1,0:T(8,128)(2,1)} %tok_hbm.1, bf16[1024,256]{1,0:T(8,128)(2,1)} %or_convert_fusion.placing, f32[256,1024]{1,0:T(8,128)} %select_add_fusion.weighting, bf16[4096,896]{1,0:T(8,128)(2,1)} %bitcast.25, bf16[4096,896]{1,0:T(8,128)(2,1)} %bitcast.26, bf16[896,4096]{1,0:T(8,128)(2,1)} %bitcast.27), custom_call_target="tpu_custom_call" | custom-call | tf_op jit(solution)/shard_map/layer/pallas_call | solution.py:344
  118.3 1.6 %copy.19 = bf16[256,256]{1,0:T(8,128)(2,1)} copy(bf16[256,256]{1,0:T(8,128)(2,1)} %layer.1) | data formatting | bytes 262144
  (5 shorter events, 0.1 us)

commit v2 on v1

v2 whole, which is shorter than its diff:
```python
import jax
import jax.numpy as jnp
from jax import lax
from jax.experimental import pallas as pl
from jax.experimental.pallas import tpu as pltpu
from jax.sharding import PartitionSpec as P

MESH = pl.DeviceIdType.MESH
REL = ((0, 0), (0, 1), (1, 0), (3, 0), (2, 0), (2, 1), (1, 1), (3, 1))
CHUNKS = (
    (0, 128, 64, False), (128, 128, 64, False), (256, 256, 192, False), (512, 256, 128, False), (768, 128, 64, True), (896, 128, 64, True),
)
F32 = jnp.float32
BF16 = jnp.bfloat16


def dot(a, b):
    return jnp.dot(a, b, preferred_element_type=F32)


def kernel(
    tok_hbm, routes, gates, gate_hbm, up_hbm, down_hbm, out_ref,
    X, Wg, Wu, Wd, tok, OB, OP, hid, part, rD, rA1, rA2, rAx, rBx, rB1, rB2, rA3, rB3, G,
    placing, whi, wlo, keys, keyr, gater, mixed,
    send_sem, recv_sem, local_sem,
):
    e = lax.axis_index("expert")
    f = lax.axis_index("ffn")
    y, xl = e // 2, e % 2
    z, xh, c = f // 4, (f // 2) % 2, f % 2
    x = xh * 2 + xl

    def at(yy, xx, zz, cc):
        yy, xx, zz = yy % 4, xx % 4, zz % 4
        return {"expert": yy * 2 + xx % 2, "ffn": zz * 4 + (xx // 2) * 2 + cc}

    loads = [
        pltpu.make_async_copy(s, d, local_sem.at[i])
        for i, (s, d) in enumerate(((tok_hbm, tok), (gate_hbm, Wg), (up_hbm, Wu), (down_hbm, Wd)))
    ]
    for cp in loads:
        cp.start()

    barrier = pltpu.get_barrier_semaphore()
    peers = [
        at(y, x, z, 1 - c), at(y, x + 1, z, c), at(y, x + 3, z, c), at(y, x + 2, z, c),
        at(y + 1, x, z, c), at(y + 3, x, z, c), at(y + 2, x, z, c),
        at(y + 1, x + 1, z, c), at(y + 1, x + 3, z, c), at(y + 3, x + 1, z, c), at(y + 3, x + 3, z, c),
        at(y + 2, x + 1, z, c), at(y + 2, x + 3, z, c), at(y, x, z + 1, c), at(y, x, z + 3, c),
        at(y, x, z + 2, c),
    ]
    for dev in peers:
        pl.semaphore_signal(barrier, inc=1, device_id=dev, device_id_type=MESH)

    expert_ids = lax.broadcasted_iota(jnp.int32, (8, 256), 0)
    first, second = routes[0:1, :] == expert_ids, routes[1:2, :] == expert_ids
    chosen = jnp.where(first | second, 1.0, 0.0)
    earlier = lax.broadcasted_iota(jnp.int32, (256, 256), 0) < lax.broadcasted_iota(jnp.int32, (256, 256), 1)
    rank = dot(chosen.astype(BF16), jnp.where(earlier, 1.0, 0.0).astype(BF16))
    keys[0] = jnp.where(first | second, rank, -1.0)
    keys[1] = jnp.where(first, gates[0:1, :], 0.0) + jnp.where(second, gates[1:2, :], 0.0)
    row_ids = lax.broadcasted_iota(jnp.int32, (128, 256), 0).astype(F32)
    for r, (dy, dx) in enumerate(REL):
        owner = ((y + 4 - dy) % 4) * 2 + (xl + dx) % 2
        key = keys[0, pl.ds(owner, 1), :]
        keyr[r:r + 1, :] = key
        gater[r:r + 1, :] = keys[1, pl.ds(owner, 1), :]
        placing[r * 128:(r + 1) * 128, :] = jnp.where(key == row_ids, 1.0, 0.0).astype(BF16)

    copies = []

    def send(src, dst, dev):
        i = len(copies)
        cp = pltpu.make_async_remote_copy(
            src_ref=src, dst_ref=dst, send_sem=send_sem.at[i], recv_sem=recv_sem.at[i],
            device_id=dev, device_id_type=MESH,
        )
        cp.start()
        copies.append(cp)
        return cp

    other = at(y, x, z, 1 - c)
    half = pl.multiple_of(c * 2048, 2048)

    def cols(b, width=256):
        return pl.ds(pl.multiple_of(b * 256, 256), width)

    x5 = (x + 1 + 2 * c) % 4
    block = c * 8 + z * 2 + xh
    block5 = c * 8 + z * 2 + x5 // 2
    loads[0].wait()
    OP[0] = dot(placing[512:640, :], tok[:, cols(block)]).astype(BF16)
    OP[1] = dot(placing[640:768, :], tok[:, cols(block5)]).astype(BF16)

    def place(lo, hi):
        def tile(t, carry):
            o = pl.multiple_of(t * 1024, 1024)
            v = dot(placing[lo:hi, :], tok[:, pl.ds(pl.multiple_of(half + o, 1024), 1024)])
            OB[lo:hi, pl.ds(o, 1024)] = v.astype(BF16)
            return carry

        lax.fori_loop(0, 2, tile, 0)

    def place_own(t, carry):
        o = pl.ds(pl.multiple_of(t * 1024, 1024), 1024)
        X[0:128, o] = dot(placing[0:128, :], tok[:, o]).astype(BF16)
        return carry

    place(128, 512)
    place(768, 1024)
    lax.fori_loop(0, 4, place_own, 0)

    pl.semaphore_wait(barrier, len(peers))

    def quarter(r, yy, i):
        return send(
            OB.at[r * 128:(r + 1) * 128, i * 1024:(i + 1) * 1024],
            X.at[r * 128:(r + 1) * 128, pl.ds(pl.multiple_of(half + i * 1024, 1024), 1024)],
            at(yy, x + 1 + 2 * i, z, c),
        )

    def send_diagonal():
        a, b = quarter(6, y + 3, 0), quarter(7, y + 1, 1)
        arrive[7] = [b, quarter(7, y + 1, 0)]
        arrive[6] = [a, quarter(6, y + 3, 1)]

    def halves(r, yy):
        rows = slice(r * 128, (r + 1) * 128)
        return [send(OB.at[rows, :], X.at[rows, pl.ds(half, 2048)], at(yy, x, z, c))]

    arrive = {}
    arrive[4] = [send(OP.at[0], X.at[512:640, cols(block)], at(y + 2, x, z, c))]
    arrive[5] = [send(OP.at[1], X.at[640:768, cols(block5)], at(y + 2, x5, z, c))]
    arrive[1] = [quarter(1, y, 0), quarter(1, y, 1)]
    arrive[2] = halves(2, y + 3)
    arrive[3] = halves(3, y + 1)

    def landed(cps):
        for cp in cps:
            cp.wait_recv()

    def forward(r):
        landed(arrive[r])
        where = X.at[r * 128:(r + 1) * 128, pl.ds(half, 2048)]
        return [send(where, where, other)]

    def spread(b, width, dev):
        where = X.at[512:768, cols(b, width)]
        return send(where, where, dev)

    pair = lambda zz: c * 8 + (zz % 4) * 2
    xdev = at(y, x + 2, z, c)
    up_z, dn_z, far_z = at(y, x, z + 1, c), at(y, x, z + 3, c), at(y, x, z + 2, c)
    gather = {}

    def gather_x():
        landed(arrive[4] + arrive[5])
        gather["x"] = [spread(block, 256, xdev)]

    def gather_z():
        landed(gather["x"])
        gather["z"] = [spread(pair(z), 512, up_z), spread(pair(z), 512, dn_z)]
        gather["core"] = [spread(pair(z), 512, other)]

    def gather_far():
        landed(gather["z"])
        gather["far"] = [spread(pair(z + 3), 256, up_z), spread(pair(z + 1) + 1, 256, dn_z)]
        gather["core"] += [spread(pair(z + 1), 512, other), spread(pair(z + 3), 512, other)]

    def gather_end():
        landed(gather["far"])
        gather["core"].append(spread(pair(z + 2), 512, other))

    def gate_up(k, lo, hi):
        rows = slice(CHUNKS[k][0], CHUNKS[k][0] + CHUNKS[k][1])
        hrows = slice(0, CHUNKS[k][1])

        def tile(t, carry):
            o = cols(t)
            g = dot(X[rows, :], Wg[:, o])
            u = dot(X[rows, :], Wu[:, o])
            hid[hrows, o] = (g / (1.0 + jnp.exp(-g)) * u).astype(BF16)
            return carry

        lax.fori_loop(lo, min(hi, 3), tile, 0)
        if hi > 3:
            w = jnp.concatenate([Wg[:, 768:896], Wu[:, 768:896]], axis=1)
            gu = dot(X[rows, :], w)
            g, u = gu[:, :128], gu[:, 128:]
            hid[hrows, 768:896] = (g / (1.0 + jnp.exp(-g)) * u).astype(BF16)

    def down(k, cc):
        row, n = CHUNKS[k][:2]

        def tile(t, carry):
            for zi in range(2):
                for xi in range(2):
                    zz = t * 2 + zi
                    v = dot(hid[0:n, :], Wd[:, cols(zz * 4 + xi * 2 + cc)])
                    part[cc, zz, xi, row:row + n, :] = v.astype(BF16)
            return carry

        lax.fori_loop(0, 2, tile, 0)

    def add(dst, *srcs):
        total = dst[...].astype(F32)
        for s in srcs:
            total = total + s[...].astype(F32)
        dst[...] = total.astype(BF16)

    zp, zm, zf = (z + 1) % 4, (z + 3) % 4, (z + 2) % 4
    mine = part.at[c]
    st = [dict() for _ in CHUNKS]

    def rows_of(k):
        row, n, a, _ = CHUNKS[k]
        mid = row + a
        return slice(row, mid), slice(mid, row + n), slice(mid, mid + (n - a) // 2), slice(mid + (n - a) // 2, row + n)

    def split(k):
        return CHUNKS[k][2] < CHUNKS[k][1]

    def direct(k):
        return CHUNKS[k][3]

    def send_core(k):
        rows = slice(CHUNKS[k][0], CHUNKS[k][0] + CHUNKS[k][1])
        st[k]["d"] = [send(part.at[1 - c, :, :, rows], rD.at[:, :, rows], other)]

    def s0(k):
        landed(st[k]["d"])
        rows = slice(CHUNKS[k][0], CHUNKS[k][0] + CHUNKS[k][1])
        a, b, _, _ = rows_of(k)

        def body(zz, carry):
            for xi in range(2):
                add(mine.at[zz, xi, rows], rD.at[zz, xi, rows])
            return carry

        lax.fori_loop(0, 4, body, 0)
        st[k]["bx"] = [send(mine.at[:, 1 - xh, b], rBx.at[:, b], xdev)] if split(k) else []
        if direct(k):
            st[k]["a2"] = [
                send(mine.at[zf, :, a], rA3.at[:, a], far_z),
                send(mine.at[zp, :, a], rA2.at[0, :, a], up_z), send(mine.at[zm, :, a], rA2.at[1, :, a], dn_z),
            ]
            return
        st[k]["a1"] = [send(mine.at[zf, 0, a], rA1.at[0, a], up_z), send(mine.at[zf, 1, a], rA1.at[1, a], dn_z)]

    def s1(k):
        a, b, lo, hi = rows_of(k)
        if direct(k):
            landed(st[k]["a2"])
            add(mine.at[z, 1 - xh, a], rA2.at[0, 1 - xh, a], rA2.at[1, 1 - xh, a], rA3.at[1 - xh, a])
            st[k]["ax"] = [send(mine.at[z, 1 - xh, a], rAx.at[a], xdev)]
            landed(st[k]["bx"])

            def body(zz, carry):
                add(mine.at[zz, xh, b], rBx.at[zz, b])
                return carry

            lax.fori_loop(0, 4, body, 0)
            st[k]["b2"] = [
                send(mine.at[zf, xh, b], rB3.at[b], far_z),
                send(mine.at[zp, xh, b], rB2.at[0, b], up_z), send(mine.at[zm, xh, b], rB2.at[1, b], dn_z),
            ]
            return
        landed(st[k]["a1"])
        add(mine.at[zp, 0, a], rA1.at[0, a])
        add(mine.at[zm, 1, a], rA1.at[1, a])
        st[k]["a2"] = [send(mine.at[zp, :, a], rA2.at[0, :, a], up_z), send(mine.at[zm, :, a], rA2.at[1, :, a], dn_z)]
        if not split(k):
            return
        landed(st[k]["bx"])

        def body(zz, carry):
            add(mine.at[zz, xh, b], rBx.at[zz, b])
            return carry

        lax.fori_loop(0, 4, body, 0)
        st[k]["b1"] = [send(mine.at[zf, xh, lo], rB1.at[lo], up_z), send(mine.at[zf, xh, hi], rB1.at[hi], dn_z)]

    def s2(k):
        a, b, lo, hi = rows_of(k)
        if split(k):
            landed(st[k]["b1"])
            add(mine.at[zp, xh, lo], rB1.at[lo])
            add(mine.at[zm, xh, hi], rB1.at[hi])
            st[k]["b2"] = [send(mine.at[zp, xh, b], rB2.at[0, b], up_z), send(mine.at[zm, xh, b], rB2.at[1, b], dn_z)]
        landed(st[k]["a2"])
        add(mine.at[z, 1 - xh, a], rA2.at[0, 1 - xh, a], rA2.at[1, 1 - xh, a])
        st[k]["ax"] = [send(mine.at[z, 1 - xh, a], rAx.at[a], xdev)]

    returned = {}

    def s3(k):
        row, n = CHUNKS[k][:2]
        a, b, _, _ = rows_of(k)
        if split(k):
            landed(st[k]["b2"])
            add(mine.at[z, xh, b], rB2.at[0, b], rB2.at[1, b], *([rB3.at[b]] if direct(k) else []))
        landed(st[k]["ax"])
        add(mine.at[z, xh, a], rA2.at[0, xh, a], rA2.at[1, xh, a], rAx.at[a], *([rA3.at[xh, a]] if direct(k) else []))
        for r in range(row // 128, (row + n) // 128):
            rows = slice(r * 128, (r + 1) * 128)
            dy, dx = REL[r]
            if r == 0:
                G[rows, :] = mine[z, xh, rows, :]
                returned[r] = []
            else:
                owner = {"expert": ((y + dy) % 4) * 2 + (xl + dx) % 2, "ffn": f}
                returned[r] = [send(mine.at[z, xh, rows], G.at[rows], owner)]

    def weigh():
        keyt, gatet = keyr[...].T, gater[...].T
        lanes = lax.broadcasted_iota(jnp.int32, (256, 128), 1).astype(F32)
        for r in range(8):
            w = jnp.where(keyt[:, r:r + 1] == lanes, gatet[:, r:r + 1], 0.0)
            hi = w.astype(BF16)
            whi[:, r * 128:(r + 1) * 128] = hi
            wlo[:, r * 128:(r + 1) * 128] = (w - hi.astype(F32)).astype(BF16)

    def combine(lo, hi):
        for r in range(lo, hi):
            landed(returned[r])
        rows = slice(lo * 128, hi * 128)
        return dot(whi[:, rows], G[rows, :]) + dot(wlo[:, rows], G[rows, :])

    loads[1].wait()
    loads[2].wait()
    gate_up(0, 0, 4)
    loads[3].wait()
    down(0, 1 - c)
    send_core(0)
    down(0, c)
    weigh()
    gather_x()
    fwd1 = forward(1)
    s0(0)
    landed(fwd1)
    gate_up(1, 0, 4)
    gather_z()
    down(1, 1 - c)
    send_core(1)
    down(1, c)
    s1(0)
    s0(1)
    fwd2 = forward(2) + forward(3)
    send_diagonal()
    landed(fwd2)
    gate_up(2, 0, 2)
    gather_far()
    gate_up(2, 2, 4)
    s1(1)
    s2(0)
    down(2, 1 - c)
    send_core(2)
    gather_end()
    down(2, c)
    s2(1)
    s0(2)
    landed(gather["core"])
    gate_up(3, 0, 4)
    s1(2)
    down(3, 1 - c)
    send_core(3)
    down(3, c)
    fwd6 = forward(6)
    fwd7 = forward(7)
    s0(3)
    landed(fwd6)
    gate_up(4, 0, 4)
    s3(0)
    s2(2)
    down(4, 1 - c)
    send_core(4)
    s3(1)
    down(4, c)
    s1(3)
    s0(4)
    landed(fwd7)
    gate_up(5, 0, 4)
    s3(2)
    s2(3)
    down(5, 1 - c)
    send_core(5)
    s1(4)
    down(5, c)
    s0(5)
    s3(3)
    mixed[...] = combine(0, 4)
    s1(5)
    s3(4)
    mixed[...] += combine(4, 6)
    s3(5)
    out_ref[...] = (mixed[...] + combine(6, 8)).astype(BF16)
    for cp in copies:
        cp.wait_send()


N_COPIES = 110


def per_device(tokens, router_gates, routes, gate_proj, up_proj, down_proj):
    rows, width = tokens.shape
    hidden = gate_proj.shape[2]
    vmem = lambda *shape: pltpu.VMEM(shape, BF16)
    any_spec = pl.BlockSpec(memory_space=pl.ANY)
    vmem_spec = pl.BlockSpec(memory_space=pltpu.VMEM)
    return pl.pallas_call(
        kernel,
        out_shape=jax.ShapeDtypeStruct((rows, 256), BF16),
        in_specs=[any_spec, vmem_spec, vmem_spec, any_spec, any_spec, any_spec],
        out_specs=vmem_spec,
        scratch_shapes=[
            vmem(1024, width), vmem(width, hidden), vmem(width, hidden), vmem(hidden, width),
            vmem(rows, width), vmem(1024, 2048), vmem(2, 128, 256), vmem(256, hidden),
            vmem(2, 4, 2, 1024, 256), vmem(4, 2, 1024, 256),
            vmem(2, 1024, 256), vmem(2, 2, 1024, 256), vmem(1024, 256),
            vmem(4, 1024, 256), vmem(1024, 256), vmem(2, 1024, 256), vmem(2, 1024, 256), vmem(1024, 256), vmem(1024, 256),
            vmem(1024, 256), vmem(256, 1024), vmem(256, 1024),
            pltpu.VMEM((2, 8, 256), F32), pltpu.VMEM((8, 256), F32), pltpu.VMEM((8, 256), F32),
            pltpu.VMEM((256, 256), F32),
            pltpu.SemaphoreType.DMA((N_COPIES,)), pltpu.SemaphoreType.DMA((N_COPIES,)),
            pltpu.SemaphoreType.DMA((4,)),
        ],
        compiler_params=pltpu.CompilerParams(
            collective_id=0, has_side_effects=True, vmem_limit_bytes=67043328
        ),
        name="layer",
    )(tokens, routes.T, router_gates.T, gate_proj[0], up_proj[0], down_proj[0])


def solution(mesh):
    in_specs = (
        P("expert", None),
        P("expert", None),
        P("expert", None),
        P("expert", None, "ffn"),
        P("expert", None, "ffn"),
        P("expert", "ffn", None),
    )
    out_specs = P("expert", "ffn")
    return jax.shard_map(
        per_device, mesh=mesh, in_specs=in_specs, out_specs=out_specs, check_vma=False
    )
```

time: 120 us -> 84.4 us (0.70)
  Pallas kernels: 112 us -> 82.2 us
  other arithmetic: 4.31 us -> 0 us
  local copies, waits for them, and re-layouts: 3.95 us -> 1.57 us
    pallas_call x1, Pallas kernels: 112 us -> 82.2 us  [per_device(): pl.pallas_call(kernel, out_shape=jax.ShapeDtypeStruct((rows, 256), BF16),...]
    add x3 -> x0, other arithmetic: 2 us -> none  [the longest x1 1.23 us: per_device(): jnp.where(first[:, None] == slot_ids[None, :], router_gates[:, 0:1], 0.0)]
where the time goes in v2:
time: 84.4 us; the launch traced here: 83.7 us
  Pallas kernels  82.2 us (97%)
  local copies, waits for them, and re-layouts  1.57 us (2%)
    pallas_call x1, Pallas kernels, per_device(): pl.pallas_call(kernel, out_shape=jax.ShapeDtypeStruct((rows, 256), BF16),...  82.2 us

profile of v2, /device:TPU:0, one launch (start us, length us, event | category | flops | bytes accessed | tf_op | source)
XLA Modules:
  0.0 83.7 jit_solution(9002018998017574481)
XLA Ops:
  0.0 82.2 %layer.1 = bf16[256,256]{1,0:T(8,128)(2,1)} custom-call(bf16[256,4096]{1,0:T(8,128)(2,1)} %tok_hbm.1, s32[2,256]{1,0:T(2,128)} %bitcast.8, f32[2,256]{1,0:T(2,128)} %bitcast.9, bf16[4096,896]{1,0:T(8,128)(2,1)} %bitcast.5, bf16[4096,896]{1,0:T(8,128)(2,1)} %bitcast.6, bf16[896,4096]{1,0:T(8,128)(2,1)} %bitcast.7), custom_call_target="tpu_custom_call" | custom-call | tf_op jit(solution)/shard_map/layer/pallas_call | solution.py:410
  82.2 1.6 %copy.8 = bf16[256,256]{1,0:T(8,128)(2,1)} copy(bf16[256,256]{1,0:T(8,128)(2,1)} %layer.1) | data formatting | bytes 262144

commit v3 on v2

v3 whole, which is shorter than its diff:
```python
import jax
import jax.numpy as jnp
from jax import lax
from jax.experimental import pallas as pl
from jax.experimental.pallas import tpu as pltpu
from jax.sharding import PartitionSpec as P

MESH = pl.DeviceIdType.MESH
REL = ((0, 0), (0, 1), (1, 0), (3, 0), (2, 1), (1, 1), (3, 1), (2, 0))
CHUNKS = (
    (0, 128, 96, False), (128, 128, 128, False), (256, 128, 128, False), (384, 128, 128, False),
    (512, 128, 96, False), (640, 128, 64, True), (768, 128, 64, True), (896, 128, 64, True),
)
F32 = jnp.float32
BF16 = jnp.bfloat16


def dot(a, b):
    return jnp.dot(a, b, preferred_element_type=F32)


def kernel(
    tok_hbm, routes_hbm, gates_hbm, gate_hbm, up_hbm, down_hbm, out_ref,
    X, Wg, Wu, Wd, tok, OB, OP, hid, part, rD, rA1, rA2, rAx, rBx, rB1, rB2, G,
    placing, whi, wlo, keys, keyr, gater, mixed, routes, gates,
    send_sem, recv_sem, local_sem,
):
    e = lax.axis_index("expert")
    f = lax.axis_index("ffn")
    y, xl = e // 2, e % 2
    z, xh, c = f // 4, (f // 2) % 2, f % 2
    x = xh * 2 + xl

    def at(yy, xx, zz, cc):
        yy, xx, zz = yy % 4, xx % 4, zz % 4
        return {"expert": yy * 2 + xx % 2, "ffn": zz * 4 + (xx // 2) * 2 + cc}

    loads = [
        pltpu.make_async_copy(s, d, local_sem.at[i])
        for i, (s, d) in enumerate((
            (tok_hbm, tok), (gate_hbm, Wg), (up_hbm, Wu), (down_hbm, Wd), (routes_hbm, routes), (gates_hbm, gates),
        ))
    ]
    for i in (4, 5, 0):
        loads[i].start()

    barrier = pltpu.get_barrier_semaphore()
    peers = [
        at(y, x, z, 1 - c), at(y, x + 1, z, c), at(y, x + 3, z, c), at(y, x + 2, z, c),
        at(y + 1, x, z, c), at(y + 3, x, z, c), at(y + 2, x, z, c),
        at(y + 1, x + 1, z, c), at(y + 1, x + 3, z, c), at(y + 3, x + 1, z, c), at(y + 3, x + 3, z, c),
        at(y + 2, x + 1, z, c), at(y + 2, x + 3, z, c), at(y, x, z + 1, c), at(y, x, z + 3, c),
        at(y, x, z + 2, c),
    ]
    for dev in peers:
        pl.semaphore_signal(barrier, inc=1, device_id=dev, device_id_type=MESH)

    loads[4].wait()
    loads[5].wait()
    expert_ids = lax.broadcasted_iota(jnp.int32, (8, 256), 0)
    first, second = routes[0:1, :] == expert_ids, routes[1:2, :] == expert_ids
    chosen = jnp.where(first | second, 1.0, 0.0)
    earlier = lax.broadcasted_iota(jnp.int32, (256, 256), 0) < lax.broadcasted_iota(jnp.int32, (256, 256), 1)
    rank = dot(chosen.astype(BF16), jnp.where(earlier, 1.0, 0.0).astype(BF16))
    keys[0] = jnp.where(first | second, rank, -1.0)
    keys[1] = jnp.where(first, gates[0:1, :], 0.0) + jnp.where(second, gates[1:2, :], 0.0)
    row_ids = lax.broadcasted_iota(jnp.int32, (128, 256), 0).astype(F32)
    for r, (dy, dx) in enumerate(REL):
        owner = ((y + 4 - dy) % 4) * 2 + (xl + dx) % 2
        key = keys[0, pl.ds(owner, 1), :]
        keyr[r:r + 1, :] = key
        gater[r:r + 1, :] = keys[1, pl.ds(owner, 1), :]
        placing[r * 128:(r + 1) * 128, :] = jnp.where(key == row_ids, 1.0, 0.0).astype(BF16)

    copies = []
    slots = {}

    def send(src, dst, dev, key):
        i = len(copies)
        if i >= N_SEND:
            copies[i - N_SEND].wait_send()
        cp = pltpu.make_async_remote_copy(
            src_ref=src, dst_ref=dst, send_sem=send_sem.at[i % N_SEND],
            recv_sem=recv_sem.at[slots.setdefault(key, len(slots))], device_id=dev, device_id_type=MESH,
        )
        cp.start()
        copies.append(cp)

    def got(key, where):
        pltpu.make_async_copy(where, where, recv_sem.at[slots[key]]).wait()

    other = at(y, x, z, 1 - c)
    half = pl.multiple_of(c * 2048, 2048)

    def cols(b, width=256):
        return pl.ds(pl.multiple_of(b * 256, 256), width)

    x4 = (x + 1 + 2 * c) % 4
    block = c * 8 + z * 2 + xh
    block4 = c * 8 + z * 2 + x4 // 2
    loads[0].wait()
    loads[1].start()
    loads[2].start()
    OP[...] = dot(placing[512:640, :], tok[:, cols(block4)]).astype(BF16)

    def place(lo, hi, to):
        def tile(t, carry):
            o = pl.multiple_of(t * 1024, 1024)
            v = dot(placing[lo:hi, :], tok[:, pl.ds(pl.multiple_of(half + o, 1024), 1024)])
            OB[to:to + hi - lo, pl.ds(o, 1024)] = v.astype(BF16)
            return carry

        lax.fori_loop(0, 2, tile, 0)

    def place_own(t, carry):
        o = pl.ds(pl.multiple_of(t * 1024, 1024), 1024)
        X[0:128, o] = dot(placing[0:128, :], tok[:, o]).astype(BF16)
        return carry

    outbox = {1: 0, 2: 128, 3: 256, 5: 384, 6: 512, 7: 640}
    place(128, 256, outbox[1])
    pl.semaphore_wait(barrier, len(peers))

    def quarter(r, yy, i):
        return send(
            OB.at[outbox[r]:outbox[r] + 128, i * 1024:(i + 1) * 1024],
            X.at[r * 128:(r + 1) * 128, pl.ds(pl.multiple_of(half + i * 1024, 1024), 1024)],
            at(yy, x + 1 + 2 * i, z, c), r,
        )

    def halves(r, yy):
        rows = slice(r * 128, (r + 1) * 128)
        send(OB.at[outbox[r]:outbox[r] + 128, :], X.at[rows, pl.ds(half, 2048)], at(yy, x, z, c), r)

    def send_diagonal():
        for r, yy, i in ((5, y + 3, 0), (6, y + 1, 1), (6, y + 1, 0), (5, y + 3, 1)):
            quarter(r, yy, i)

    send(OP, X.at[512:640, cols(block4)], at(y + 2, x4, z, c), 4)
    quarter(1, y, 0)
    quarter(1, y, 1)
    place(256, 512, outbox[2])
    halves(2, y + 3)
    halves(3, y + 1)
    loads[3].start()
    place(640, 1024, outbox[5])
    lax.fori_loop(0, 4, place_own, 0)

    def half_rows(lo, hi):
        return X.at[lo * 128:hi * 128, pl.ds(half, 2048)]

    def forward(lo, hi):
        for r in range(lo, hi):
            got(r, half_rows(r, r + 1))
        send(half_rows(lo, hi), half_rows(lo, hi), other, ("core", lo))

    def forwarded(lo, hi):
        got(("core", lo), half_rows(lo, hi))

    def spread(b, width, dev, key):
        where = X.at[512:640, cols(b, width)]
        send(where, where, dev, key)

    pair = lambda zz: c * 8 + (zz % 4) * 2
    xdev = at(y, x + 2, z, c)
    up_z, dn_z, far_z = at(y, x, z + 1, c), at(y, x, z + 3, c), at(y, x, z + 2, c)

    def gather_x():
        got(4, OP)
        spread(block, 256, xdev, "x")

    def gather_z():
        got("x", X.at[512:640, 0:256])
        spread(pair(z), 512, up_z, "z")
        spread(pair(z), 512, dn_z, "z")
        spread(pair(z), 512, other, "c")

    def gather_far():
        got("z", X.at[512:640, 0:1024])
        spread(pair(z + 3), 256, up_z, "far")
        spread(pair(z + 1) + 1, 256, dn_z, "far")
        spread(pair(z + 1), 512, other, "c")
        spread(pair(z + 3), 512, other, "c")

    def gather_end():
        got("far", X.at[512:640, 0:512])
        spread(pair(z + 2), 512, other, "c")

    def gathered():
        got("c", half_rows(4, 5))

    def gate_up(k, lo, hi):
        rows = slice(CHUNKS[k][0], CHUNKS[k][0] + CHUNKS[k][1])
        hrows = slice(0, CHUNKS[k][1])

        def tile(t, carry):
            o = cols(t)
            g = dot(X[rows, :], Wg[:, o])
            u = dot(X[rows, :], Wu[:, o])
            hid[hrows, o] = (g / (1.0 + jnp.exp(-g)) * u).astype(BF16)
            return carry

        lax.fori_loop(lo, min(hi, 3), tile, 0)
        if hi > 3:
            w = jnp.concatenate([Wg[:, 768:896], Wu[:, 768:896]], axis=1)
            gu = dot(X[rows, :], w)
            g, u = gu[:, :128], gu[:, 128:]
            hid[hrows, 768:896] = (g / (1.0 + jnp.exp(-g)) * u).astype(BF16)

    def down(k, cc):
        row, n = CHUNKS[k][:2]

        def tile(t, carry):
            for zi in range(2):
                for xi in range(2):
                    zz = t * 2 + zi
                    v = dot(hid[0:n, :], Wd[:, cols(zz * 4 + xi * 2 + cc)])
                    part[cc, zz, xi, row:row + n, :] = v.astype(BF16)
            return carry

        lax.fori_loop(0, 2, tile, 0)

    def down_other(k):
        rows = slice(CHUNKS[k][0], CHUNKS[k][0] + CHUNKS[k][1])
        down(k, 1 - c)
        send(part.at[1 - c, :, :, rows], rD.at[:, :, rows], other, ("d", k))

    def down_own(k):
        down(k, c)

    def add(dst, *srcs):
        total = dst[...].astype(F32)
        for s in srcs:
            total = total + s[...].astype(F32)
        dst[...] = total.astype(BF16)

    zp, zm, zf = (z + 1) % 4, (z + 3) % 4, (z + 2) % 4
    mine = part.at[c]

    def rows_of(k):
        row, n, a, _ = CHUNKS[k]
        mid = row + a
        return slice(row, mid), slice(mid, row + n), slice(mid, mid + (n - a) // 2), slice(mid + (n - a) // 2, row + n)

    def split(k):
        return CHUNKS[k][2] < CHUNKS[k][1]

    def direct(k):
        return CHUNKS[k][3]

    def s0(k):
        rows = slice(CHUNKS[k][0], CHUNKS[k][0] + CHUNKS[k][1])
        got(("d", k), rD.at[:, :, rows])
        a, b, _, _ = rows_of(k)

        def body(zz, carry):
            for xi in range(2):
                add(mine.at[zz, xi, rows], rD.at[zz, xi, rows])
            return carry

        lax.fori_loop(0, 4, body, 0)
        if split(k):
            send(mine.at[:, 1 - xh, b], rBx.at[:, b], xdev, ("bx", k))
        if direct(k):
            send(mine.at[zf, :, a], rA2.at[2, :, a], far_z, ("a2", k))
            send(mine.at[zp, :, a], rA2.at[0, :, a], up_z, ("a2", k))
            send(mine.at[zm, :, a], rA2.at[1, :, a], dn_z, ("a2", k))
        else:
            send(mine.at[zf, 0, a], rA1.at[0, a], up_z, ("a1", k))
            send(mine.at[zf, 1, a], rA1.at[1, a], dn_z, ("a1", k))

    def z_terms(k):
        return range(3 if direct(k) else 2)

    def x_first(k):
        _, b, lo, hi = rows_of(k)
        got(("bx", k), rBx.at[:, b])

        def body(zz, carry):
            add(mine.at[zz, xh, b], rBx.at[zz, b])
            return carry

        lax.fori_loop(0, 4, body, 0)
        if direct(k):
            send(mine.at[zf, xh, b], rB2.at[2, b], far_z, ("b2", k))
            send(mine.at[zp, xh, b], rB2.at[0, b], up_z, ("b2", k))
            send(mine.at[zm, xh, b], rB2.at[1, b], dn_z, ("b2", k))
        else:
            send(mine.at[zf, xh, lo], rB1.at[lo], up_z, ("b1", k))
            send(mine.at[zf, xh, hi], rB1.at[hi], dn_z, ("b1", k))

    def z_sum(k):
        a = rows_of(k)[0]
        got(("a2", k), rA2.at[0:len(z_terms(k)), :, a])
        add(mine.at[z, 1 - xh, a], *[rA2.at[i, 1 - xh, a] for i in z_terms(k)])
        send(mine.at[z, 1 - xh, a], rAx.at[a], xdev, ("ax", k))

    def s1(k):
        a = rows_of(k)[0]
        if direct(k):
            z_sum(k)
        else:
            got(("a1", k), rA1.at[:, a])
            add(mine.at[zp, 0, a], rA1.at[0, a])
            add(mine.at[zm, 1, a], rA1.at[1, a])
            send(mine.at[zp, :, a], rA2.at[0, :, a], up_z, ("a2", k))
            send(mine.at[zm, :, a], rA2.at[1, :, a], dn_z, ("a2", k))
        if split(k):
            x_first(k)

    def s2(k):
        _, b, lo, hi = rows_of(k)
        if split(k):
            got(("b1", k), rB1.at[b])
            add(mine.at[zp, xh, lo], rB1.at[lo])
            add(mine.at[zm, xh, hi], rB1.at[hi])
            send(mine.at[zp, xh, b], rB2.at[0, b], up_z, ("b2", k))
            send(mine.at[zm, xh, b], rB2.at[1, b], dn_z, ("b2", k))
        z_sum(k)

    def s3(k):
        row, n = CHUNKS[k][:2]
        a, b, _, _ = rows_of(k)
        if split(k):
            got(("b2", k), rB2.at[0:len(z_terms(k)), b])
            add(mine.at[z, xh, b], *[rB2.at[i, b] for i in z_terms(k)])
        got(("ax", k), rAx.at[a])
        add(mine.at[z, xh, a], rAx.at[a], *[rA2.at[i, xh, a] for i in z_terms(k)])
        for r in range(row // 128, (row + n) // 128):
            rows = slice(r * 128, (r + 1) * 128)
            dy, dx = REL[r]
            if r == 0:
                G[rows, :] = mine[z, xh, rows, :]
            else:
                owner = {"expert": ((y + dy) % 4) * 2 + (xl + dx) % 2, "ffn": f}
                send(mine.at[z, xh, rows], G.at[rows], owner, ("back", k))

    def weigh():
        keyt, gatet = keyr[...].T, gater[...].T
        lanes = lax.broadcasted_iota(jnp.int32, (256, 128), 1).astype(F32)
        for r in range(8):
            w = jnp.where(keyt[:, r:r + 1] == lanes, gatet[:, r:r + 1], 0.0)
            hi = w.astype(BF16)
            whi[:, r * 128:(r + 1) * 128] = hi
            wlo[:, r * 128:(r + 1) * 128] = (w - hi.astype(F32)).astype(BF16)

    def combine(k):
        rows = slice(CHUNKS[k][0], CHUNKS[k][0] + CHUNKS[k][1])
        if k:
            got(("back", k), G.at[rows])
        return dot(whi[:, rows], G[rows, :]) + dot(wlo[:, rows], G[rows, :])

    loads[1].wait()
    loads[2].wait()
    gate_up(0, 0, 4)
    loads[3].wait()
    down_other(0)
    down_own(0)
    weigh()
    gather_x()
    forward(1, 2)
    s0(0)
    forwarded(1, 2)
    gate_up(1, 0, 4)
    gather_z()
    down_other(1)
    down_own(1)
    forward(2, 3)
    forward(3, 4)
    send_diagonal()
    s0(1)
    forwarded(2, 3)
    gate_up(2, 0, 2)
    s1(0)
    gate_up(2, 2, 4)
    gather_far()
    down_other(2)
    down_own(2)
    forwarded(3, 4)
    gate_up(3, 0, 2)
    s0(2)
    s1(1)
    gate_up(3, 2, 4)
    gather_end()
    down_other(3)
    s2(0)
    halves(7, y + 2)
    down_own(3)
    gathered()
    gate_up(4, 0, 2)
    s0(3)
    s1(2)
    gate_up(4, 2, 4)
    down_other(4)
    s2(1)
    forward(5, 7)
    down_own(4)
    forwarded(5, 7)
    gate_up(5, 0, 2)
    s0(4)
    s1(3)
    gate_up(5, 2, 4)
    down_other(5)
    s2(2)
    s3(0)
    down_own(5)
    gate_up(6, 0, 2)
    s0(5)
    s1(4)
    gate_up(6, 2, 4)
    down_other(6)
    s2(3)
    s3(1)
    forward(7, 8)
    down_own(6)
    forwarded(7, 8)
    gate_up(7, 0, 2)
    s0(6)
    gate_up(7, 2, 4)
    s1(5)
    down_other(7)
    s2(4)
    s3(2)
    down_own(7)
    s0(7)
    s3(3)
    mixed[...] = combine(0) + combine(1) + combine(2)
    s1(6)
    s3(4)
    s3(5)
    s1(7)
    s3(6)
    mixed[...] += combine(3) + combine(4)
    s3(7)
    mixed[...] += combine(5) + combine(6)
    out_ref[...] = (mixed[...] + combine(7)).astype(BF16)
    assert len(slots) == N_RECV
    for cp in copies[-N_SEND:]:
        cp.wait_send()


N_SEND = 20
N_RECV = 64


def per_device(tokens, router_gates, routes, gate_proj, up_proj, down_proj):
    rows, width = tokens.shape
    hidden = gate_proj.shape[2]
    vmem = lambda *shape: pltpu.VMEM(shape, BF16)
    return pl.pallas_call(
        kernel,
        out_shape=jax.ShapeDtypeStruct((rows, 256), BF16),
        in_specs=[pl.BlockSpec(memory_space=pltpu.HBM)] * 6,
        out_specs=pl.BlockSpec(memory_space=pltpu.VMEM),
        scratch_shapes=[
            vmem(1024, width), vmem(width, hidden), vmem(width, hidden), vmem(hidden, width),
            vmem(rows, width), vmem(768, 2048), vmem(128, 256), vmem(256, hidden),
            vmem(2, 4, 2, 1024, 256), vmem(4, 2, 1024, 256),
            vmem(2, 1024, 256), vmem(3, 2, 1024, 256), vmem(1024, 256),
            vmem(4, 1024, 256), vmem(1024, 256), vmem(3, 1024, 256), vmem(1024, 256),
            vmem(1024, 256), vmem(256, 1024), vmem(256, 1024),
            pltpu.VMEM((2, 8, 256), F32), pltpu.VMEM((8, 256), F32), pltpu.VMEM((8, 256), F32),
            pltpu.VMEM((256, 256), F32), pltpu.VMEM((2, 256), jnp.int32), pltpu.VMEM((2, 256), F32),
            pltpu.SemaphoreType.DMA((N_SEND,)), pltpu.SemaphoreType.DMA((N_RECV,)),
            pltpu.SemaphoreType.DMA((6,)),
        ],
        compiler_params=pltpu.CompilerParams(
            collective_id=0, has_side_effects=True, vmem_limit_bytes=66 * 10**6
        ),
        name="layer",
    )(tokens, routes.T, router_gates.T, gate_proj[0], up_proj[0], down_proj[0])


def solution(mesh):
    in_specs = (
        P("expert", None),
        P("expert", None),
        P("expert", None),
        P("expert", None, "ffn"),
        P("expert", None, "ffn"),
        P("expert", "ffn", None),
    )
    out_specs = P("expert", "ffn")
    return jax.shard_map(
        per_device, mesh=mesh, in_specs=in_specs, out_specs=out_specs, check_vma=False
    )
```

time: 84.4 us -> 78.8 us (0.934)
  Pallas kernels: 82.2 us -> 77.1 us
    pallas_call x1, Pallas kernels: 82.2 us -> 77.1 us  [per_device(): pl.pallas_call(kernel, out_shape=jax.ShapeDtypeStruct((rows, 256), BF16),...]
where the time goes in v3:
time: 78.8 us; the launch traced here: 78.7 us
  Pallas kernels  77.1 us (98%)
  local copies, waits for them, and re-layouts  1.57 us (2%)
    pallas_call x1, Pallas kernels, per_device(): pl.pallas_call(kernel, out_shape=jax.ShapeDtypeStruct((rows, 256), BF16),...  77.1 us

profile of v3, /device:TPU:0, one launch (start us, length us, event | category | flops | bytes accessed | tf_op | source)
XLA Modules:
  0.0 78.7 jit_solution(7419559059194113319)
XLA Ops:
  0.0 77.1 %layer.1 = bf16[256,256]{1,0:T(8,128)(2,1)} custom-call(bf16[256,4096]{1,0:T(8,128)(2,1)} %tok_hbm.1, s32[2,256]{1,0:T(2,128)} %bitcast.8, f32[2,256]{1,0:T(2,128)} %bitcast.9, bf16[4096,896]{1,0:T(8,128)(2,1)} %bitcast.5, bf16[4096,896]{1,0:T(8,128)(2,1)} %bitcast.6, bf16[896,4096]{1,0:T(8,128)(2,1)} %bitcast.7), custom_call_target="tpu_custom_call" | custom-call | tf_op jit(solution)/shard_map/layer/pallas_call | solution.py:450
  77.1 1.6 %copy.8 = bf16[256,256]{1,0:T(8,128)(2,1)} copy(bf16[256,256]{1,0:T(8,128)(2,1)} %layer.1) | data formatting | bytes 262144

commit v4 on v3

--- a/solution.py
+++ b/solution.py
@@ -6,10 +6,10 @@
 from jax.sharding import PartitionSpec as P
 
 MESH = pl.DeviceIdType.MESH
-REL = ((0, 0), (0, 1), (1, 0), (3, 0), (2, 1), (1, 1), (3, 1), (2, 0))
+REL = ((0, 0), (0, 1), (1, 0), (3, 0), (2, 1), (2, 0), (1, 1), (3, 1))
 CHUNKS = (
     (0, 128, 96, False), (128, 128, 128, False), (256, 128, 128, False), (384, 128, 128, False),
-    (512, 128, 96, False), (640, 128, 64, True), (768, 128, 64, True), (896, 128, 64, True),
+    (512, 128, 64, False), (768, 128, 48, True), (896, 128, 64, True), (640, 128, 64, True),
 )
 F32 = jnp.float32
 BF16 = jnp.bfloat16
@@ -101,7 +101,8 @@
     loads[0].wait()
     loads[1].start()
     loads[2].start()
-    OP[...] = dot(placing[512:640, :], tok[:, cols(block4)]).astype(BF16)
+    OP[0:128, :] = dot(placing[512:640, :], tok[:, cols(block4)]).astype(BF16)
+    OP[128:192, :] = dot(placing[640:704, :], tok[:, cols(block)]).astype(BF16)
 
     def place(lo, hi, to):
         def tile(t, carry):
@@ -117,7 +118,7 @@
         X[0:128, o] = dot(placing[0:128, :], tok[:, o]).astype(BF16)
         return carry
 
-    outbox = {1: 0, 2: 128, 3: 256, 5: 384, 6: 512, 7: 640}
+    outbox = {1: 0, 2: 128, 3: 256, 6: 448, 7: 576}
     place(128, 256, outbox[1])
     pl.semaphore_wait(barrier, len(peers))
 
@@ -133,32 +134,44 @@
         send(OB.at[outbox[r]:outbox[r] + 128, :], X.at[rows, pl.ds(half, 2048)], at(yy, x, z, c), r)
 
     def send_diagonal():
-        for r, yy, i in ((5, y + 3, 0), (6, y + 1, 1), (6, y + 1, 0), (5, y + 3, 1)):
+        for r, yy, i in ((6, y + 3, 0), (7, y + 1, 1), (7, y + 1, 0), (6, y + 3, 1)):
             quarter(r, yy, i)
 
-    send(OP, X.at[512:640, cols(block4)], at(y + 2, x4, z, c), 4)
+    send(OP.at[0:128], X.at[512:640, cols(block4)], at(y + 2, x4, z, c), 4)
+    send(OP.at[128:192], X.at[640:704, cols(block)], at(y + 2, x, z, c), 5)
     quarter(1, y, 0)
     quarter(1, y, 1)
     place(256, 512, outbox[2])
     halves(2, y + 3)
     halves(3, y + 1)
     loads[3].start()
-    place(640, 1024, outbox[5])
+    place(704, 1024, 384)
     lax.fori_loop(0, 4, place_own, 0)
 
     def half_rows(lo, hi):
         return X.at[lo * 128:hi * 128, pl.ds(half, 2048)]
 
-    def forward(lo, hi):
-        for r in range(lo, hi):
-            got(r, half_rows(r, r + 1))
-        send(half_rows(lo, hi), half_rows(lo, hi), other, ("core", lo))
-
-    def forwarded(lo, hi):
-        got(("core", lo), half_rows(lo, hi))
+    def forward(r):
+        got(r, half_rows(r, r + 1))
+        send(half_rows(r, r + 1), half_rows(r, r + 1), other, ("core", r))
+
+    def forwarded(r):
+        got(("core", r), half_rows(r, r + 1))
+
+    last = X.at[704:768, pl.ds(half, 2048)]
+
+    def send_last():
+        send(OB.at[384:448, :], last, at(y + 2, x, z, c), "last")
+
+    def forward_last():
+        got("last", last)
+        send(last, last, other, ("core", 5))
+
+    def forwarded_last():
+        got(("core", 5), last)
 
     def spread(b, width, dev, key):
-        where = X.at[512:640, cols(b, width)]
+        where = X.at[512:704, cols(b, width)]
         send(where, where, dev, key)
 
     pair = lambda zz: c * 8 + (zz % 4) * 2
@@ -166,59 +179,43 @@
     up_z, dn_z, far_z = at(y, x, z + 1, c), at(y, x, z + 3, c), at(y, x, z + 2, c)
 
     def gather_x():
-        got(4, OP)
+        got(4, OP.at[0:128])
+        got(5, OP.at[128:192])
         spread(block, 256, xdev, "x")
 
     def gather_z():
-        got("x", X.at[512:640, 0:256])
+        got("x", X.at[512:704, 0:256])
         spread(pair(z), 512, up_z, "z")
         spread(pair(z), 512, dn_z, "z")
         spread(pair(z), 512, other, "c")
 
     def gather_far():
-        got("z", X.at[512:640, 0:1024])
+        got("z", X.at[512:704, 0:1024])
         spread(pair(z + 3), 256, up_z, "far")
         spread(pair(z + 1) + 1, 256, dn_z, "far")
         spread(pair(z + 1), 512, other, "c")
         spread(pair(z + 3), 512, other, "c")
 
     def gather_end():
-        got("far", X.at[512:640, 0:512])
+        got("far", X.at[512:704, 0:512])
         spread(pair(z + 2), 512, other, "c")
 
     def gathered():
-        got("c", half_rows(4, 5))
+        got("c", X.at[512:704, pl.ds(half, 2048)])
 
     def gate_up(k, lo, hi):
-        rows = slice(CHUNKS[k][0], CHUNKS[k][0] + CHUNKS[k][1])
-        hrows = slice(0, CHUNKS[k][1])
-
-        def tile(t, carry):
-            o = cols(t)
-            g = dot(X[rows, :], Wg[:, o])
-            u = dot(X[rows, :], Wu[:, o])
-            hid[hrows, o] = (g / (1.0 + jnp.exp(-g)) * u).astype(BF16)
-            return carry
-
-        lax.fori_loop(lo, min(hi, 3), tile, 0)
-        if hi > 3:
-            w = jnp.concatenate([Wg[:, 768:896], Wu[:, 768:896]], axis=1)
-            gu = dot(X[rows, :], w)
-            g, u = gu[:, :128], gu[:, 128:]
-            hid[hrows, 768:896] = (g / (1.0 + jnp.exp(-g)) * u).astype(BF16)
+        row, n = CHUNKS[k][:2]
+        w = jnp.concatenate([Wg[:, lo:hi], Wu[:, lo:hi]], axis=1)
+        both = dot(X[row:row + n, :], w)
+        g, u = both[:, :hi - lo], both[:, hi - lo:]
+        hid[0:n, lo:hi] = (g / (1.0 + jnp.exp(-g)) * u).astype(BF16)
 
     def down(k, cc):
         row, n = CHUNKS[k][:2]
-
-        def tile(t, carry):
-            for zi in range(2):
-                for xi in range(2):
-                    zz = t * 2 + zi
-                    v = dot(hid[0:n, :], Wd[:, cols(zz * 4 + xi * 2 + cc)])
-                    part[cc, zz, xi, row:row + n, :] = v.astype(BF16)
-            return carry
-
-        lax.fori_loop(0, 2, tile, 0)
+        w = jnp.concatenate([Wd[:, cols(b * 2 + cc)] for b in range(8)], axis=1)
+        v = dot(hid[0:n, :], w).astype(BF16)
+        for b in range(8):
+            part[cc, b // 2, b % 2, row:row + n, :] = v[:, b * 256:(b + 1) * 256]
 
     def down_other(k):
         rows = slice(CHUNKS[k][0], CHUNKS[k][0] + CHUNKS[k][1])
@@ -350,73 +347,78 @@
             got(("back", k), G.at[rows])
         return dot(whi[:, rows], G[rows, :]) + dot(wlo[:, rows], G[rows, :])
 
+    A, B = (0, 512), (512, 896)
     loads[1].wait()
     loads[2].wait()
-    gate_up(0, 0, 4)
+    gate_up(0, *A)
+    gate_up(0, *B)
     loads[3].wait()
     down_other(0)
     down_own(0)
+    gather_x()
     weigh()
-    gather_x()
-    forward(1, 2)
+    forward(1)
     s0(0)
-    forwarded(1, 2)
-    gate_up(1, 0, 4)
+    forwarded(1)
+    gate_up(1, *A)
     gather_z()
+    gate_up(1, *B)
     down_other(1)
     down_own(1)
-    forward(2, 3)
-    forward(3, 4)
+    s1(0)
+    forward(2)
+    forward(3)
     send_diagonal()
     s0(1)
-    forwarded(2, 3)
-    gate_up(2, 0, 2)
-    s1(0)
-    gate_up(2, 2, 4)
+    forwarded(2)
+    gate_up(2, *A)
     gather_far()
+    gate_up(2, *B)
     down_other(2)
     down_own(2)
-    forwarded(3, 4)
-    gate_up(3, 0, 2)
+    s1(1)
+    s2(0)
+    forwarded(3)
+    gate_up(3, *A)
     s0(2)
-    s1(1)
-    gate_up(3, 2, 4)
+    gate_up(3, *B)
     gather_end()
     down_other(3)
-    s2(0)
-    halves(7, y + 2)
+    send_last()
     down_own(3)
     gathered()
-    gate_up(4, 0, 2)
+    gate_up(4, *A)
     s0(3)
     s1(2)
-    gate_up(4, 2, 4)
+    gate_up(4, *B)
     down_other(4)
     s2(1)
-    forward(5, 7)
     down_own(4)
-    forwarded(5, 7)
-    gate_up(5, 0, 2)
+    forward(6)
+    forward(7)
     s0(4)
+    forwarded(6)
+    gate_up(5, *A)
     s1(3)
-    gate_up(5, 2, 4)
+    gate_up(5, *B)
     down_other(5)
     s2(2)
     s3(0)
     down_own(5)
-    gate_up(6, 0, 2)
+    forwarded(7)
+    gate_up(6, *A)
     s0(5)
     s1(4)
-    gate_up(6, 2, 4)
+    forward_last()
+    gate_up(6, *B)
     down_other(6)
     s2(3)
     s3(1)
-    forward(7, 8)
     down_own(6)
-    forwarded(7, 8)
-    gate_up(7, 0, 2)
+    forwarded_last()
+    gate_up(7, *A)
     s0(6)
-    gate_up(7, 2, 4)
+    gate_up(7, *B)
     s1(5)
     down_other(7)
     s2(4)
@@ -430,9 +432,9 @@
     s3(5)
     s1(7)
     s3(6)
-    mixed[...] += combine(3) + combine(4)
     s3(7)
-    mixed[...] += combine(5) + combine(6)
+    mixed[...] += combine(3) + combine(4) + combine(5)
+    mixed[...] += combine(6)
     out_ref[...] = (mixed[...] + combine(7)).astype(BF16)
     assert len(slots) == N_RECV
     for cp in copies[-N_SEND:]:
@@ -440,7 +442,7 @@
 
 
 N_SEND = 20
-N_RECV = 64
+N_RECV = 66
 
 
 def per_device(tokens, router_gates, routes, gate_proj, up_proj, down_proj):
@@ -454,7 +456,7 @@
         out_specs=pl.BlockSpec(memory_space=pltpu.VMEM),
         scratch_shapes=[
             vmem(1024, width), vmem(width, hidden), vmem(width, hidden), vmem(hidden, width),
-            vmem(rows, width), vmem(768, 2048), vmem(128, 256), vmem(256, hidden),
+            vmem(rows, width), vmem(704, 2048), vmem(192, 256), vmem(256, hidden),
             vmem(2, 4, 2, 1024, 256), vmem(4, 2, 1024, 256),
             vmem(2, 1024, 256), vmem(3, 2, 1024, 256), vmem(1024, 256),
             vmem(4, 1024, 256), vmem(1024, 256), vmem(3, 1024, 256), vmem(1024, 256),

time: 78.8 us -> 75.7 us (0.961)
  Pallas kernels: 77.1 us -> 73.9 us
    pallas_call x1, Pallas kernels: 77.1 us -> 73.9 us  [per_device(): pl.pallas_call(kernel, out_shape=jax.ShapeDtypeStruct((rows, 256), BF16),...]
where the time goes in v4:
time: 75.7 us; the launch traced here: 75.5 us
  Pallas kernels  73.9 us (98%)
  local copies, waits for them, and re-layouts  1.57 us (2%)
    pallas_call x1, Pallas kernels, per_device(): pl.pallas_call(kernel, out_shape=jax.ShapeDtypeStruct((rows, 256), BF16),...  73.9 us
    unnamed x1, local copies, waits for them, and re-layouts  1.57 us

profile of v4, /device:TPU:0, one launch (start us, length us, event | category | flops | bytes accessed | tf_op | source)
XLA Modules:
  0.0 75.5 jit_solution(11600665429272098400)
XLA Ops:
  0.0 73.9 %layer.1 = bf16[256,256]{1,0:T(8,128)(2,1)} custom-call(bf16[256,4096]{1,0:T(8,128)(2,1)} %tok_hbm.1, s32[2,256]{1,0:T(2,128)} %bitcast.8, f32[2,256]{1,0:T(2,128)} %bitcast.9, bf16[4096,896]{1,0:T(8,128)(2,1)} %bitcast.5, bf16[4096,896]{1,0:T(8,128)(2,1)} %bitcast.6, bf16[896,4096]{1,0:T(8,128)(2,1)} %bitcast.7), custom_call_target="tpu_custom_call" | custom-call | tf_op jit(solution)/shard_map/layer/pallas_call | solution.py:452
  73.9 1.6 %copy.8 = bf16[256,256]{1,0:T(8,128)(2,1)} copy(bf16[256,256]{1,0:T(8,128)(2,1)} %layer.1) | data formatting | bytes 262144

commit v5 on v4

--- a/solution.py
+++ b/solution.py
@@ -393,12 +393,12 @@
     gate_up(4, *B)
     down_other(4)
     s2(1)
+    forward(6)
     down_own(4)
-    forward(6)
     forward(7)
-    s0(4)
     forwarded(6)
     gate_up(5, *A)
+    s0(4)
     s1(3)
     gate_up(5, *B)
     down_other(5)
@@ -426,11 +426,11 @@
     down_own(7)
     s0(7)
     s3(3)
-    mixed[...] = combine(0) + combine(1) + combine(2)
     s1(6)
     s3(4)
     s3(5)
     s1(7)
+    mixed[...] = combine(0) + combine(1) + combine(2)
     s3(6)
     s3(7)
     mixed[...] += combine(3) + combine(4) + combine(5)

time: 75.7 us -> 76 us (level)
  no operation moved by 1% of the time
where the time goes in v5:
time: 76 us; the launch traced here: 75.8 us
  Pallas kernels  74.2 us (98%)
  local copies, waits for them, and re-layouts  1.57 us (2%)
    pallas_call x1, Pallas kernels, per_device(): pl.pallas_call(kernel, out_shape=jax.ShapeDtypeStruct((rows, 256), BF16),...  74.2 us
    unnamed x1, local copies, waits for them, and re-layouts  1.57 us

profile of v5, /device:TPU:0, one launch (start us, length us, event | category | flops | bytes accessed | tf_op | source)
XLA Modules:
  0.0 75.8 jit_solution(4600771112132153661)
XLA Ops:
  0.0 74.2 %layer.1 = bf16[256,256]{1,0:T(8,128)(2,1)} custom-call(bf16[256,4096]{1,0:T(8,128)(2,1)} %tok_hbm.1, s32[2,256]{1,0:T(2,128)} %bitcast.8, f32[2,256]{1,0:T(2,128)} %bitcast.9, bf16[4096,896]{1,0:T(8,128)(2,1)} %bitcast.5, bf16[4096,896]{1,0:T(8,128)(2,1)} %bitcast.6, bf16[896,4096]{1,0:T(8,128)(2,1)} %bitcast.7), custom_call_target="tpu_custom_call" | custom-call | tf_op jit(solution)/shard_map/layer/pallas_call | solution.py:452
  74.3 1.6 %copy.8 = bf16[256,256]{1,0:T(8,128)(2,1)} copy(bf16[256,256]{1,0:T(8,128)(2,1)} %layer.1) | data formatting | bytes 262144
